TPU v7x, 32 devices: a whole 2x2x4 slice. The times are simulated.
32 devices in a mesh: lat: 8 (over y, x, core), lon: 4 (over z).
Axes of the slice: x: 2, y: 2, z: 4, core: 2. Of those that a mesh axis runs over, the one named last changes fastest.
Arguments:
- inputs: bfloat16 [128, 384, 256], P('lat', 'lon'), may hold values from -6 to 6
- first_filter: bfloat16 [3, 3, 256, 256], replicated, may hold values from -0.125 to 0.125
- second_filter: bfloat16 [3, 3, 256, 256], replicated, may hold values from -0.125 to 0.125
- cotangent: bfloat16 [128, 384, 256], P('lat', 'lon'), may hold values from -30 to 30
Outputs:
- input_grad: bfloat16 [128, 384, 256], P('lat', 'lon')
- first_grad: float32 [3, 3, 256, 256], replicated
- second_grad: float32 [3, 3, 256, 256], replicated
All inputs are finite; a program needn't handle non-finite values.
Results may differ from a plain program's by a relative error of at most 0.0061.
Values may be sent and summed in bfloat16 or wider, within the bound.
A program may use at most 64 MiB of HBM per device.

v0:
```python
import jax
import jax.numpy as jnp
from jax import lax
from jax.sharding import PartitionSpec as P


def extended(block, sides, width):
    for axis, dim in sides:
        count = lax.axis_size(axis)
        forward = [(i, i + 1) for i in range(count - 1)]
        forward.append((count - 1, 0))
        backward = [(target, source) for source, target in forward]
        low = lax.ppermute(
            lax.slice_in_dim(block, block.shape[dim] - width, None, axis=dim), axis, forward
        )
        high = lax.ppermute(lax.slice_in_dim(block, 0, width, axis=dim), axis, backward)
        block = jnp.concatenate([low, block, high], axis=dim)
    return block


def mask_rows(padded, width):
    rows = padded.shape[0] - 2 * width
    position = lax.broadcasted_iota(jnp.int32, (padded.shape[0], 1, 1), 0)
    index = lax.axis_index("lat")
    count = lax.axis_size("lat")
    dropped = (position < width) & (index == 0) | (position >= rows + width) & (index == count - 1)
    return jnp.where(dropped, jnp.zeros((), padded.dtype), padded)


def extend(field):
    padded = extended(field, (("lat", 0), ("lon", 1)), 1)
    return mask_rows(padded, 1)


def conv_taps(padded, weight, rows, cols, flipped):
    total = jnp.zeros(
        (rows * cols, weight.shape[3] if not flipped else weight.shape[2]), jnp.float32
    )
    for first in range(3):
        for second in range(3):
            piece = padded[first : first + rows, second : second + cols, :].reshape(rows * cols, -1)
            if flipped:
                total = total + lax.dot_general(
                    piece,
                    weight[2 - first, 2 - second],
                    (((1,), (1,)), ((), ())),
                    preferred_element_type=jnp.float32,
                )
            else:
                total = total + jnp.dot(
                    piece, weight[first, second], preferred_element_type=jnp.float32
                )
    return total.reshape(rows, cols, -1)


def filter_grad(padded, delta, rows, cols):
    flat = delta.reshape(rows * cols, -1)
    taps = []
    for first in range(3):
        for second in range(3):
            piece = padded[first : first + rows, second : second + cols, :].reshape(rows * cols, -1)
            taps.append(
                lax.dot_general(
                    piece, flat, (((0,), (0,)), ((), ())), preferred_element_type=jnp.float32
                )
            )
    return jnp.stack(taps).reshape(3, 3, flat.shape[1], flat.shape[1])


def gelu_value(value):
    return value * 0.5 * (1.0 + jax.scipy.special.erf(value * 0.7071067811865476))


def gelu_slope(value):
    return (
        0.5 * (1.0 + jax.scipy.special.erf(value * 0.7071067811865476))
        + value * jnp.exp(-0.5 * value * value) * 0.3989422804014327
    )


def body(inputs, first_filter, second_filter, cotangent):
    rows, cols = (inputs.shape[0], inputs.shape[1])
    padded_in = extend(inputs)
    hidden_one = conv_taps(padded_in, first_filter, rows, cols, False)
    act = gelu_value(hidden_one).astype(jnp.bfloat16)
    padded_act = extend(act)
    hidden_two = conv_taps(padded_act, second_filter, rows, cols, False)
    delta_two = (cotangent.astype(jnp.float32) * gelu_slope(hidden_two)).astype(jnp.bfloat16)
    second_part = filter_grad(padded_act, delta_two, rows, cols)
    act_grad = conv_taps(extend(delta_two), second_filter, rows, cols, True)
    delta_one = (act_grad * gelu_slope(hidden_one)).astype(jnp.bfloat16)
    first_part = filter_grad(padded_in, delta_one, rows, cols)
    first_grad, second_grad = lax.psum((first_part, second_part), ("lat", "lon"))
    input_grad = conv_taps(extend(delta_one), first_filter, rows, cols, True).astype(jnp.bfloat16)
    return (input_grad, first_grad, second_grad)


def solution(mesh):
    in_specs = (P("lat", "lon", None), P(), P(), P("lat", "lon", None))
    out_specs = (P("lat", "lon", None), P(), P())
    return jax.shard_map(body, mesh=mesh, in_specs=in_specs, out_specs=out_specs, check_vma=False)
```

profile of v0, /device:TPU:0, one launch (start us, length us, event | category | flops | bytes accessed | tf_op | source)
XLA Modules:
  0.0 228.8 jit_solution(7460417335077282387)
XLA Ops:
  8.6 2.9 %collective-permute-start.1 = (bf16[1,96,256]{2,1,0:T(8,128)(2,1)S(1)}, bf16[1,96,256]{2,1,0:T(8,128)(2,1)S(1)}, u32[]{:S(2)}, u32[]{:S(2)}) collective-permute-start(bf16[1,96,256]{2,1,0:T(8,128)(2,1)S(1)} %get-tuple-element.55), channel_id=1, source_target_pairs={{4,0},{8,4},{12,8},{16,12},{20,16},{24,20},{28,24},{0,28},{5,1},{9... | collective-permute-start | bytes 147464 | tf_op jit(solution)/shard_map/ppermute | solution.py:16
  11.5 1.7 collective-permute-done
  13.2 1.2 constant_dynamic-update-slice_fusion.1
  14.5 4.4 %collective-permute-start.3 = (bf16[18,1,256]{2,1,0:T(2,128)(2,1)S(1)}, bf16[18,1,256]{2,1,0:T(2,128)(2,1)S(1)}, u32[]{:S(2)}, u32[]{:S(2)}) collective-permute-start(bf16[18,1,256]{2,1,0:T(2,128)(2,1)S(1)} %get-tuple-element.48), channel_id=1, source_target_pairs={{1,0},{2,1},{3,2},{0,3},{5,4},{6,5},{7,6},{4,7},{9,8},{10,9},{11,1... | collective-permute-start | bytes 27656 | tf_op jit(solution)/shard_map/ppermute | solution.py:16
  18.9 1.5 collective-permute-done.3
  20.3 4.1 %collective-permute-done.2 = bf16[18,1,256]{2,1,0:T(2,128)(2,1)S(1)} collective-permute-done((bf16[18,1,256]{2,1,0:T(2,128)(2,1)S(1)}, bf16[18,1,256]{2,1,0:T(2,128)(2,1)S(1)}, u32[]{:S(2)}, u32[]{:S(2)}) %collective-permute-start.2) | collective-permute-done | bytes 9248 | tf_op jit(solution)/shard_map/ppermute | solution.py:13
  30.5 1.4 collective-permute-done.5
  31.9 2.6 %collective-permute-done.4 = bf16[1,96,256]{2,1,0:T(8,128)(2,1)S(1)} collective-permute-done((bf16[1,96,256]{2,1,0:T(8,128)(2,1)S(1)}, bf16[1,96,256]{2,1,0:T(8,128)(2,1)S(1)}, u32[]{:S(2)}, u32[]{:S(2)}) %collective-permute-start.4) | collective-permute-done | bytes 49184 | tf_op jit(solution)/shard_map/ppermute | solution.py:13
  34.8 1.8 collective-permute-start.6
  36.6 1.7 collective-permute-done.7
  38.4 2.0 collective-permute-done.6
  51.0 1.1 collective-permute-done.8
  52.2 2.0 collective-permute-start.10
  54.7 1.3 collective-permute-done.11
  56.0 1.9 collective-permute-done.10
  58.4 1.1 fusion.126
  67.8 1.4 collective-permute-done.12
  69.3 2.0 collective-permute-start.14
  71.8 1.4 copy-done.4
  73.2 2.0 collective-permute-done.14
  80.1 1.3 fusion
  81.4 135.8 %all-reduce.3.cloned.1.call-done = (f32[3,3,256,256]{3,2,1,0:T(8,128)}, f32[3,3,256,256]{3,2,1,0:T(8,128)}) async-done(((f32[3,3,256,256]{3,2,1,0:T(8,128)}, f32[3,3,256,256]{3,2,1,0:T(8,128)}), (f32[3,3,256,256]{3,2,1,0:T(8,128)}, f32[3,3,256,256]{3,2,1,0:T(8,128)})) %all-reduce.3.cloned.1.call-update) | async-done | bytes 4718608 | tf_op jit(solution)/shard_map/psum | solution.py:93
  217.2 3.4 %copy.27 = f32[3,3,256,256]{3,2,1,0:T(8,128)} copy(f32[3,3,256,256]{3,2,1,0:T(8,128)} %get-tuple-element.58) | data formatting | bytes 4718592
  220.5 1.4 copy.28
  (102 shorter events, 32.9 us)
Async XLA Ops:
  7.2 210.0 %all-reduce.3.cloned.1.call-start = ((), (), s32[]{:S(2)}) async-start(), calls=%async_computation | async-start | bytes 9437184 | tf_op jit(solution)/shard_map/psum | solution.py:93
  8.0 5.2 %collective-permute-start = (bf16[1,96,256]{2,1,0:T(8,128)(2,1)S(1)}, bf16[1,96,256]{2,1,0:T(8,128)(2,1)S(1)}, u32[]{:S(2)}, u32[]{:S(2)}) collective-permute-start(bf16[1,96,256]{2,1,0:T(8,128)(2,1)S(1)} %get-tuple-element.56), channel_id=1, source_target_pairs={{0,4},{4,8},{8,12},{12,16},{16,20},{20,24},{24,28},{28,0},{1,5},{5... | collective-permute-start | bytes 147464 | tf_op jit(solution)/shard_map/ppermute | solution.py:13
  8.6 5.8 %collective-permute-start.1 = (bf16[1,96,256]{2,1,0:T(8,128)(2,1)S(1)}, bf16[1,96,256]{2,1,0:T(8,128)(2,1)S(1)}, u32[]{:S(2)}, u32[]{:S(2)}) collective-permute-start(bf16[1,96,256]{2,1,0:T(8,128)(2,1)S(1)} %get-tuple-element.55), channel_id=1, source_target_pairs={{4,0},{8,4},{12,8},{16,12},{20,16},{24,20},{28,24},{0,28},{5,1},{9... | collective-permute-start | bytes 147464 | tf_op jit(solution)/shard_map/ppermute | solution.py:16
  14.5 5.9 %collective-permute-start.3 = (bf16[18,1,256]{2,1,0:T(2,128)(2,1)S(1)}, bf16[18,1,256]{2,1,0:T(2,128)(2,1)S(1)}, u32[]{:S(2)}, u32[]{:S(2)}) collective-permute-start(bf16[18,1,256]{2,1,0:T(2,128)(2,1)S(1)} %get-tuple-element.48), channel_id=1, source_target_pairs={{1,0},{2,1},{3,2},{0,3},{5,4},{6,5},{7,6},{4,7},{9,8},{10,9},{11,1... | collective-permute-start | bytes 27656 | tf_op jit(solution)/shard_map/ppermute | solution.py:16
  18.9 5.6 %collective-permute-start.2 = (bf16[18,1,256]{2,1,0:T(2,128)(2,1)S(1)}, bf16[18,1,256]{2,1,0:T(2,128)(2,1)S(1)}, u32[]{:S(2)}, u32[]{:S(2)}) collective-permute-start(bf16[18,1,256]{2,1,0:T(2,128)(2,1)S(1)} %get-tuple-element.47), channel_id=1, source_target_pairs={{0,1},{1,2},{2,3},{3,0},{4,5},{5,6},{6,7},{7,4},{8,9},{9,10},{10,1... | collective-permute-start | bytes 27656 | tf_op jit(solution)/shard_map/ppermute | solution.py:13
  25.0 1.3 copy-start.1
  30.0 2.0 collective-permute-start.5
  30.0 4.5 %collective-permute-start.4 = (bf16[1,96,256]{2,1,0:T(8,128)(2,1)S(1)}, bf16[1,96,256]{2,1,0:T(8,128)(2,1)S(1)}, u32[]{:S(2)}, u32[]{:S(2)}) collective-permute-start(bf16[1,96,256]{2,1,0:T(8,128)(2,1)S(1)} %get-tuple-element.53), channel_id=1, source_target_pairs={{0,4},{4,8},{8,12},{12,16},{16,20},{20,24},{24,28},{28,0},{1,5},{5... | collective-permute-start | bytes 147464 | tf_op jit(solution)/shard_map/ppermute | solution.py:13
  34.5 3.8 %collective-permute-start.7 = (bf16[18,1,256]{2,1,0:T(2,128)(2,1)S(1)}, bf16[18,1,256]{2,1,0:T(2,128)(2,1)S(1)}, u32[]{:S(2)}, u32[]{:S(2)}) collective-permute-start(bf16[18,1,256]{2,1,0:T(2,128)(2,1)S(1)} %get-tuple-element.46), channel_id=1, source_target_pairs={{1,0},{2,1},{3,2},{0,3},{5,4},{6,5},{7,6},{4,7},{9,8},{10,9},{11,1... | collective-permute-start | bytes 27656 | tf_op jit(solution)/shard_map/ppermute | solution.py:16
  34.8 5.6 %collective-permute-start.6 = (bf16[18,1,256]{2,1,0:T(2,128)(2,1)S(1)}, bf16[18,1,256]{2,1,0:T(2,128)(2,1)S(1)}, u32[]{:S(2)}, u32[]{:S(2)}) collective-permute-start(bf16[18,1,256]{2,1,0:T(2,128)(2,1)S(1)} %get-tuple-element.45), channel_id=1, source_target_pairs={{0,1},{1,2},{2,3},{3,0},{4,5},{5,6},{6,7},{7,4},{8,9},{9,10},{10,1... | collective-permute-start | bytes 27656 | tf_op jit(solution)/shard_map/ppermute | solution.py:13
  40.9 1.3 copy-start
  45.1 1.1 copy-start.5
  47.4 3.6 %collective-permute-start.9 = (bf16[1,96,256]{2,1,0:T(8,128)(2,1)S(1)}, bf16[1,96,256]{2,1,0:T(8,128)(2,1)S(1)}, u32[]{:S(2)}, u32[]{:S(2)}) collective-permute-start(bf16[1,96,256]{2,1,0:T(8,128)(2,1)S(1)} %get-tuple-element.52), channel_id=1, source_target_pairs={{4,0},{8,4},{12,8},{16,12},{20,16},{24,20},{28,24},{0,28},{5,1},{9... | collective-permute-start | bytes 147464 | tf_op jit(solution)/shard_map/ppermute | solution.py:16
  47.5 4.6 %collective-permute-start.8 = (bf16[1,96,256]{2,1,0:T(8,128)(2,1)S(1)}, bf16[1,96,256]{2,1,0:T(8,128)(2,1)S(1)}, u32[]{:S(2)}, u32[]{:S(2)}) collective-permute-start(bf16[1,96,256]{2,1,0:T(8,128)(2,1)S(1)} %get-tuple-element.51), channel_id=1, source_target_pairs={{0,4},{4,8},{8,12},{12,16},{16,20},{20,24},{24,28},{28,0},{1,5},{5... | collective-permute-start | bytes 147464 | tf_op jit(solution)/shard_map/ppermute | solution.py:13
  52.2 3.8 %collective-permute-start.11 = (bf16[18,1,256]{2,1,0:T(2,128)(2,1)S(1)}, bf16[18,1,256]{2,1,0:T(2,128)(2,1)S(1)}, u32[]{:S(2)}, u32[]{:S(2)}) collective-permute-start(bf16[18,1,256]{2,1,0:T(2,128)(2,1)S(1)} %get-tuple-element.44), channel_id=1, source_target_pairs={{1,0},{2,1},{3,2},{0,3},{5,4},{6,5},{7,6},{4,7},{9,8},{10,9},{11,1... | collective-permute-start | bytes 27656 | tf_op jit(solution)/shard_map/ppermute | solution.py:16
  52.2 5.6 %collective-permute-start.10 = (bf16[18,1,256]{2,1,0:T(2,128)(2,1)S(1)}, bf16[18,1,256]{2,1,0:T(2,128)(2,1)S(1)}, u32[]{:S(2)}, u32[]{:S(2)}) collective-permute-start(bf16[18,1,256]{2,1,0:T(2,128)(2,1)S(1)} %get-tuple-element.43), channel_id=1, source_target_pairs={{0,1},{1,2},{2,3},{3,0},{4,5},{5,6},{6,7},{7,4},{8,9},{9,10},{10,1... | collective-permute-start | bytes 27656 | tf_op jit(solution)/shard_map/ppermute | solution.py:13
  54.7 4.8 %copy-start.3 = (f32[9,256,256]{2,1,0:T(8,128)}, f32[9,256,256]{2,1,0:T(8,128)S(1)}, u32[]{:S(2)}) copy-start(f32[9,256,256]{2,1,0:T(8,128)S(1)} %fusion.13) | copy-start | bytes 7077892
  64.2 3.6 %collective-permute-start.13 = (bf16[1,96,256]{2,1,0:T(8,128)(2,1)S(1)}, bf16[1,96,256]{2,1,0:T(8,128)(2,1)S(1)}, u32[]{:S(2)}, u32[]{:S(2)}) collective-permute-start(bf16[1,96,256]{2,1,0:T(8,128)(2,1)S(1)} %get-tuple-element.50), channel_id=1, source_target_pairs={{4,0},{8,4},{12,8},{16,12},{20,16},{24,20},{28,24},{0,28},{5,1},{9... | collective-permute-start | bytes 147464 | tf_op jit(solution)/shard_map/ppermute | solution.py:16
  64.8 4.4 %collective-permute-start.12 = (bf16[1,96,256]{2,1,0:T(8,128)(2,1)S(1)}, bf16[1,96,256]{2,1,0:T(8,128)(2,1)S(1)}, u32[]{:S(2)}, u32[]{:S(2)}) collective-permute-start(bf16[1,96,256]{2,1,0:T(8,128)(2,1)S(1)} %get-tuple-element.49), channel_id=1, source_target_pairs={{0,4},{4,8},{8,12},{12,16},{16,20},{20,24},{24,28},{28,0},{1,5},{5... | collective-permute-start | bytes 147464 | tf_op jit(solution)/shard_map/ppermute | solution.py:13
  69.2 3.9 %collective-permute-start.15 = (bf16[18,1,256]{2,1,0:T(2,128)(2,1)S(1)}, bf16[18,1,256]{2,1,0:T(2,128)(2,1)S(1)}, u32[]{:S(2)}, u32[]{:S(2)}) collective-permute-start(bf16[18,1,256]{2,1,0:T(2,128)(2,1)S(1)} %get-tuple-element.42), channel_id=1, source_target_pairs={{1,0},{2,1},{3,2},{0,3},{5,4},{6,5},{7,6},{4,7},{9,8},{10,9},{11,1... | collective-permute-start | bytes 27656 | tf_op jit(solution)/shard_map/ppermute | solution.py:16
  69.3 5.8 %collective-permute-start.14 = (bf16[18,1,256]{2,1,0:T(2,128)(2,1)S(1)}, bf16[18,1,256]{2,1,0:T(2,128)(2,1)S(1)}, u32[]{:S(2)}, u32[]{:S(2)}) collective-permute-start(bf16[18,1,256]{2,1,0:T(2,128)(2,1)S(1)} %get-tuple-element.41), channel_id=1, source_target_pairs={{0,1},{1,2},{2,3},{3,0},{4,5},{5,6},{6,7},{7,4},{8,9},{9,10},{10,1... | collective-permute-start | bytes 27656 | tf_op jit(solution)/shard_map/ppermute | solution.py:13
  71.7 1.4 copy-start.4
  217.2 3.4 %copy-start.2 = (f32[3,3,256,256]{3,2,1,0:T(8,128)S(1)}, f32[3,3,256,256]{3,2,1,0:T(8,128)}, u32[]{:S(2)}) copy-start(f32[3,3,256,256]{3,2,1,0:T(8,128)} %get-tuple-element.59) | copy-start | bytes 7077892
Sparse Core Ops, SparseCore 0:
  73.3 143.8 all-reduce.2
where the time goes:
time: 229 us
  waiting for transfers between devices  158 us (69%)
  matrix products  22.3 us (10%)
  starting transfers between devices  15.8 us (7%)
  between operations  14.6 us (6%)
  local copies, waits for them, and re-layouts  13.6 us (6%)
  other arithmetic  4.03 us (2%)
    psum x1, waiting for transfers between devices, body(): lax.psum((first_part, second_part), ('lat', 'lon'))  136 us
    ppermute x8, waiting for transfers between devices, extended(): lax.ppermute(lax.slice_in_dim(block, block.shape[dim] - width, None, axis...  16.7 us
    unnamed x16, local copies, waits for them, and re-layouts  8.77 us
    ppermute x8, starting transfers between devices, extended(): lax.ppermute(lax.slice_in_dim(block, 0, width, axis=dim), axis, backward)  8.4 us
    dot_general x18, matrix products, conv_taps(): lax.dot_general(piece, weight[2 - first, 2 - second], (((1,), (1,)), ((),...  8.18 us
    dot_general x18, matrix products, filter_grad(): lax.dot_general(piece, flat, (((0,), (0,)), ((), ())), preferred_element_...  7.54 us
    ppermute x8, starting transfers between devices, extended(): lax.ppermute(lax.slice_in_dim(block, block.shape[dim] - width, None, axis...  7.38 us
    dot_general x18, matrix products, conv_taps(): jnp.dot(piece, weight[first, second], preferred_element_type=jnp.float32)  6.59 us
  transfers between devices with their start and end apart: 17, of which 13 were waited for; matrix products, arithmetic and copies ran while one was open for 6% of the time, Pallas kernels for 0%

commit v1 on v0

--- a/solution.py
+++ b/solution.py
@@ -2,6 +2,7 @@
 import jax.numpy as jnp
 from jax import lax
 from jax.sharding import PartitionSpec as P
+from jax.lax import psum
 
 
 def extended(block, sides, width):
@@ -90,7 +91,13 @@
     act_grad = conv_taps(extend(delta_two), second_filter, rows, cols, True)
     delta_one = (act_grad * gelu_slope(hidden_one)).astype(jnp.bfloat16)
     first_part = filter_grad(padded_in, delta_one, rows, cols)
-    first_grad, second_grad = lax.psum((first_part, second_part), ("lat", "lon"))
+
+    def part_paths(vals):
+        for m in ("lon", "lat"):
+            vals = psum(vals, m)
+        return vals
+
+    first_grad, second_grad = part_paths((first_part, second_part))
     input_grad = conv_taps(extend(delta_one), first_filter, rows, cols, True).astype(jnp.bfloat16)
     return (input_grad, first_grad, second_grad)
 

time: 229 us -> 341 us (1.49)
  waiting for transfers between devices: 158 us -> 263 us
  local copies, waits for them, and re-layouts: 13.6 us -> 19.3 us
    psum x1 -> x2, waiting for transfers between devices: 136 us -> 235 us  [part_paths(): vals = psum(vals, m)]
    ppermute x8, waiting for transfers between devices: 5.89 us -> 9.86 us  [extended(): lax.ppermute(lax.slice_in_dim(block, 0, width, axis=dim), axis, backward)]
    unnamed x16 -> x28, local copies, waits for them, and re-layouts: 8.77 us -> 12.2 us
  transfers between devices with their start and end apart: 17 -> 18, of which waited for: 13 -> 16; matrix products, arithmetic and copies ran while one was open for 6% -> 4% of each run, Pallas kernels for 0% -> 0%
where the time goes in v1:
time: 341 us; the launch traced here: 340 us
  waiting for transfers between devices  263 us (77%)
  matrix products  23.5 us (7%)
  local copies, waits for them, and re-layouts  19.3 us (6%)
  starting transfers between devices  15.9 us (5%)
  between operations  14.6 us (4%)
  other arithmetic  4.07 us (1%)
    psum x2, waiting for transfers between devices, part_paths(): vals = psum(vals, m)  235 us
    ppermute x8, waiting for transfers between devices, extended(): lax.ppermute(lax.slice_in_dim(block, block.shape[dim] - width, None, axis...  18 us
    unnamed x28, local copies, waits for them, and re-layouts  12.2 us
    ppermute x8, waiting for transfers between devices, extended(): lax.ppermute(lax.slice_in_dim(block, 0, width, axis=dim), axis, backward)  9.86 us
    dot_general x18, matrix products, conv_taps(): lax.dot_general(piece, weight[2 - first, 2 - second], (((1,), (1,)), ((),...  9.24 us
    ppermute x8, starting transfers between devices, extended(): lax.ppermute(lax.slice_in_dim(block, 0, width, axis=dim), axis, backward)  8.35 us
    dot_general x18, matrix products, filter_grad(): lax.dot_general(piece, flat, (((0,), (0,)), ((), ())), preferred_element_...  7.53 us
    ppermute x8, starting transfers between devices, extended(): lax.ppermute(lax.slice_in_dim(block, block.shape[dim] - width, None, axis...  7.43 us
  transfers between devices with their start and end apart: 18, of which 16 were waited for; matrix products, arithmetic and copies ran while one was open for 4% of the time, Pallas kernels for 0%

profile of v1, /device:TPU:0, one launch (start us, length us, event | category | flops | bytes accessed | tf_op | source)
XLA Modules:
  0.0 339.9 jit_solution(12427262720204764210)
XLA Ops:
  8.6 2.9 collective-permute-start.1
  11.5 1.7 collective-permute-done
  14.5 4.4 %collective-permute-start.3 = (bf16[18,1,256]{2,1,0:T(2,128)(2,1)S(1)}, bf16[18,1,256]{2,1,0:T(2,128)(2,1)S(1)}, u32[]{:S(2)}, u32[]{:S(2)}) collective-permute-start(bf16[18,1,256]{2,1,0:T(2,128)(2,1)S(1)} %get-tuple-element.50), channel_id=1, source_target_pairs={{1,0},{2,1},{3,2},{0,3},{5,4},{6,5},{7,6},{4,7},{9,8},{10,9},{11,1... | collective-permute-start | bytes 27656 | tf_op jit(solution)/shard_map/ppermute | solution.py:17
  18.9 1.5 collective-permute-done.3
  20.3 4.1 %collective-permute-done.2 = bf16[18,1,256]{2,1,0:T(2,128)(2,1)S(1)} collective-permute-done((bf16[18,1,256]{2,1,0:T(2,128)(2,1)S(1)}, bf16[18,1,256]{2,1,0:T(2,128)(2,1)S(1)}, u32[]{:S(2)}, u32[]{:S(2)}) %collective-permute-start.2) | collective-permute-done | bytes 9248 | tf_op jit(solution)/shard_map/ppermute | solution.py:14
  30.6 1.4 collective-permute-done.5
  32.1 2.6 collective-permute-done.4
  34.8 1.9 collective-permute-start.6
  36.7 1.7 collective-permute-done.7
  38.5 1.9 collective-permute-done.6
  52.3 2.0 collective-permute-start.10
  56.1 1.9 collective-permute-done.10
  67.6 1.4 copy-done.10
  69.7 1.7 collective-permute-done.13
  71.4 2.7 collective-permute-done.12
  74.2 2.0 collective-permute-start.14
  76.2 2.3 collective-permute-done.15
  78.4 2.1 collective-permute-done.14
  81.1 3.1 fusion.125
  84.6 154.7 %all-reduce.7.cloned.1.call-done = (f32[3,3,256,256]{3,2,1,0:T(8,128)}, f32[3,3,256,256]{3,2,1,0:T(8,128)}) async-done(((f32[3,3,256,256]{3,2,1,0:T(8,128)}, f32[3,3,256,256]{3,2,1,0:T(8,128)}), (f32[3,3,256,256]{3,2,1,0:T(8,128)}, f32[3,3,256,256]{3,2,1,0:T(8,128)})) %all-reduce.7.cloned.1.call-update) | async-done | bytes 4718608 | tf_op jit(solution)/shard_map/psum | solution.py:97
  239.4 1.6 convolution_add_fusion.7
  248.4 80.0 %all-reduce.5.cloned.1.call-done = (f32[3,3,256,256]{3,2,1,0:T(8,128)}, f32[3,3,256,256]{3,2,1,0:T(8,128)}) async-done(((f32[3,3,256,256]{3,2,1,0:T(8,128)}, f32[3,3,256,256]{3,2,1,0:T(8,128)}), (f32[3,3,256,256]{3,2,1,0:T(8,128)}, f32[3,3,256,256]{3,2,1,0:T(8,128)})) %all-reduce.5.cloned.1.call-update) | async-done | bytes 4718608 | tf_op jit(solution)/shard_map/psum | solution.py:97
  328.3 3.4 copy.29
  331.7 1.4 copy.30
  (117 shorter events, 41.0 us)
Async XLA Ops:
  7.2 232.2 %all-reduce.7.cloned.1.call-start = ((), (), s32[]{:S(2)}) async-start(), calls=%async_computation.1 | async-start | bytes 9437184 | tf_op jit(solution)/shard_map/psum | solution.py:97
  8.0 5.2 %collective-permute-start = (bf16[1,96,256]{2,1,0:T(8,128)(2,1)S(1)}, bf16[1,96,256]{2,1,0:T(8,128)(2,1)S(1)}, u32[]{:S(2)}, u32[]{:S(2)}) collective-permute-start(bf16[1,96,256]{2,1,0:T(8,128)(2,1)S(1)} %get-tuple-element.58), channel_id=1, source_target_pairs={{0,4},{4,8},{8,12},{12,16},{16,20},{20,24},{24,28},{28,0},{1,5},{5... | collective-permute-start | bytes 147464 | tf_op jit(solution)/shard_map/ppermute | solution.py:14
  8.6 5.8 %collective-permute-start.1 = (bf16[1,96,256]{2,1,0:T(8,128)(2,1)S(1)}, bf16[1,96,256]{2,1,0:T(8,128)(2,1)S(1)}, u32[]{:S(2)}, u32[]{:S(2)}) collective-permute-start(bf16[1,96,256]{2,1,0:T(8,128)(2,1)S(1)} %get-tuple-element.57), channel_id=1, source_target_pairs={{4,0},{8,4},{12,8},{16,12},{20,16},{24,20},{28,24},{0,28},{5,1},{9... | collective-permute-start | bytes 147464 | tf_op jit(solution)/shard_map/ppermute | solution.py:17
  14.5 5.9 %collective-permute-start.3 = (bf16[18,1,256]{2,1,0:T(2,128)(2,1)S(1)}, bf16[18,1,256]{2,1,0:T(2,128)(2,1)S(1)}, u32[]{:S(2)}, u32[]{:S(2)}) collective-permute-start(bf16[18,1,256]{2,1,0:T(2,128)(2,1)S(1)} %get-tuple-element.50), channel_id=1, source_target_pairs={{1,0},{2,1},{3,2},{0,3},{5,4},{6,5},{7,6},{4,7},{9,8},{10,9},{11,1... | collective-permute-start | bytes 27656 | tf_op jit(solution)/shard_map/ppermute | solution.py:17
  18.9 5.6 %collective-permute-start.2 = (bf16[18,1,256]{2,1,0:T(2,128)(2,1)S(1)}, bf16[18,1,256]{2,1,0:T(2,128)(2,1)S(1)}, u32[]{:S(2)}, u32[]{:S(2)}) collective-permute-start(bf16[18,1,256]{2,1,0:T(2,128)(2,1)S(1)} %get-tuple-element.49), channel_id=1, source_target_pairs={{0,1},{1,2},{2,3},{3,0},{4,5},{5,6},{6,7},{7,4},{8,9},{9,10},{10,1... | collective-permute-start | bytes 27656 | tf_op jit(solution)/shard_map/ppermute | solution.py:14
  25.0 1.3 copy-start.1
  30.1 2.0 collective-permute-start.5
  30.1 4.5 %collective-permute-start.4 = (bf16[1,96,256]{2,1,0:T(8,128)(2,1)S(1)}, bf16[1,96,256]{2,1,0:T(8,128)(2,1)S(1)}, u32[]{:S(2)}, u32[]{:S(2)}) collective-permute-start(bf16[1,96,256]{2,1,0:T(8,128)(2,1)S(1)} %get-tuple-element.55), channel_id=1, source_target_pairs={{0,4},{4,8},{8,12},{12,16},{16,20},{20,24},{24,28},{28,0},{1,5},{5... | collective-permute-start | bytes 147464 | tf_op jit(solution)/shard_map/ppermute | solution.py:14
  34.6 3.8 %collective-permute-start.7 = (bf16[18,1,256]{2,1,0:T(2,128)(2,1)S(1)}, bf16[18,1,256]{2,1,0:T(2,128)(2,1)S(1)}, u32[]{:S(2)}, u32[]{:S(2)}) collective-permute-start(bf16[18,1,256]{2,1,0:T(2,128)(2,1)S(1)} %get-tuple-element.48), channel_id=1, source_target_pairs={{1,0},{2,1},{3,2},{0,3},{5,4},{6,5},{7,6},{4,7},{9,8},{10,9},{11,1... | collective-permute-start | bytes 27656 | tf_op jit(solution)/shard_map/ppermute | solution.py:17
  34.8 5.6 %collective-permute-start.6 = (bf16[18,1,256]{2,1,0:T(2,128)(2,1)S(1)}, bf16[18,1,256]{2,1,0:T(2,128)(2,1)S(1)}, u32[]{:S(2)}, u32[]{:S(2)}) collective-permute-start(bf16[18,1,256]{2,1,0:T(2,128)(2,1)S(1)} %get-tuple-element.47), channel_id=1, source_target_pairs={{0,1},{1,2},{2,3},{3,0},{4,5},{5,6},{6,7},{7,4},{8,9},{9,10},{10,1... | collective-permute-start | bytes 27656 | tf_op jit(solution)/shard_map/ppermute | solution.py:14
  41.0 1.3 copy-start
  47.5 3.6 %collective-permute-start.9 = (bf16[1,96,256]{2,1,0:T(8,128)(2,1)S(1)}, bf16[1,96,256]{2,1,0:T(8,128)(2,1)S(1)}, u32[]{:S(2)}, u32[]{:S(2)}) collective-permute-start(bf16[1,96,256]{2,1,0:T(8,128)(2,1)S(1)} %get-tuple-element.54), channel_id=1, source_target_pairs={{4,0},{8,4},{12,8},{16,12},{20,16},{24,20},{28,24},{0,28},{5,1},{9... | collective-permute-start | bytes 147464 | tf_op jit(solution)/shard_map/ppermute | solution.py:17
  47.6 4.6 %collective-permute-start.8 = (bf16[1,96,256]{2,1,0:T(8,128)(2,1)S(1)}, bf16[1,96,256]{2,1,0:T(8,128)(2,1)S(1)}, u32[]{:S(2)}, u32[]{:S(2)}) collective-permute-start(bf16[1,96,256]{2,1,0:T(8,128)(2,1)S(1)} %get-tuple-element.53), channel_id=1, source_target_pairs={{0,4},{4,8},{8,12},{12,16},{16,20},{20,24},{24,28},{28,0},{1,5},{5... | collective-permute-start | bytes 147464 | tf_op jit(solution)/shard_map/ppermute | solution.py:14
  52.2 3.8 %collective-permute-start.11 = (bf16[18,1,256]{2,1,0:T(2,128)(2,1)S(1)}, bf16[18,1,256]{2,1,0:T(2,128)(2,1)S(1)}, u32[]{:S(2)}, u32[]{:S(2)}) collective-permute-start(bf16[18,1,256]{2,1,0:T(2,128)(2,1)S(1)} %get-tuple-element.46), channel_id=1, source_target_pairs={{1,0},{2,1},{3,2},{0,3},{5,4},{6,5},{7,6},{4,7},{9,8},{10,9},{11,1... | collective-permute-start | bytes 27656 | tf_op jit(solution)/shard_map/ppermute | solution.py:17
  52.3 5.6 %collective-permute-start.10 = (bf16[18,1,256]{2,1,0:T(2,128)(2,1)S(1)}, bf16[18,1,256]{2,1,0:T(2,128)(2,1)S(1)}, u32[]{:S(2)}, u32[]{:S(2)}) collective-permute-start(bf16[18,1,256]{2,1,0:T(2,128)(2,1)S(1)} %get-tuple-element.45), channel_id=1, source_target_pairs={{0,1},{1,2},{2,3},{3,0},{4,5},{5,6},{6,7},{7,4},{8,9},{9,10},{10,1... | collective-permute-start | bytes 27656 | tf_op jit(solution)/shard_map/ppermute | solution.py:14
  54.8 4.7 %copy-start.9 = (f32[9,256,256]{2,1,0:T(8,128)}, f32[9,256,256]{2,1,0:T(8,128)S(1)}, u32[]{:S(2)}) copy-start(f32[9,256,256]{2,1,0:T(8,128)S(1)} %fusion.13) | copy-start | bytes 7077892
  67.6 1.4 copy-start.10
  69.0 259.3 %all-reduce.5.cloned.1.call-start = ((), (), s32[]{:S(2)}) async-start(), calls=%async_computation | async-start | bytes 9437184 | tf_op jit(solution)/shard_map/psum | solution.py:97
  69.1 2.3 collective-permute-start.13
  69.6 4.4 %collective-permute-start.12 = (bf16[1,96,256]{2,1,0:T(8,128)(2,1)S(1)}, bf16[1,96,256]{2,1,0:T(8,128)(2,1)S(1)}, u32[]{:S(2)}, u32[]{:S(2)}) collective-permute-start(bf16[1,96,256]{2,1,0:T(8,128)(2,1)S(1)} %get-tuple-element.51), channel_id=1, source_target_pairs={{0,4},{4,8},{8,12},{12,16},{16,20},{20,24},{24,28},{28,0},{1,5},{5... | collective-permute-start | bytes 147464 | tf_op jit(solution)/shard_map/ppermute | solution.py:14
  74.1 4.3 %collective-permute-start.15 = (bf16[18,1,256]{2,1,0:T(2,128)(2,1)S(1)}, bf16[18,1,256]{2,1,0:T(2,128)(2,1)S(1)}, u32[]{:S(2)}, u32[]{:S(2)}) collective-permute-start(bf16[18,1,256]{2,1,0:T(2,128)(2,1)S(1)} %get-tuple-element.44), channel_id=1, source_target_pairs={{1,0},{2,1},{3,2},{0,3},{5,4},{6,5},{7,6},{4,7},{9,8},{10,9},{11,1... | collective-permute-start | bytes 27656 | tf_op jit(solution)/shard_map/ppermute | solution.py:17
  74.2 6.3 %collective-permute-start.14 = (bf16[18,1,256]{2,1,0:T(2,128)(2,1)S(1)}, bf16[18,1,256]{2,1,0:T(2,128)(2,1)S(1)}, u32[]{:S(2)}, u32[]{:S(2)}) collective-permute-start(bf16[18,1,256]{2,1,0:T(2,128)(2,1)S(1)} %get-tuple-element.43), channel_id=1, source_target_pairs={{0,1},{1,2},{2,3},{3,0},{4,5},{5,6},{6,7},{7,4},{8,9},{9,10},{10,1... | collective-permute-start | bytes 27656 | tf_op jit(solution)/shard_map/ppermute | solution.py:14
  239.4 1.6 copy-start.7
  328.3 3.4 copy-start.8
  (6 other events, 6.8 us)
Sparse Core Ops, SparseCore 0:
  69.2 170.1 all-reduce.6
  242.7 85.5 all-reduce.4
